TPU v7x, 32 devices: a whole 2x2x4 slice. The times are simulated.
32 devices in a mesh: grp: 2 (over y), row: 4 (over x, core), col: 4 (over z).
Axes of the slice: x: 2, y: 2, z: 4, core: 2. Of those that a mesh axis runs over, the one named last changes fastest.
Arguments:
- perturbation: bfloat16 [4, 12000, 12000], P('grp', 'row', 'col'), parts along dimension 0, may hold values from -96 to 96
- occ_coeffs: bfloat16 [12000, 2000], P('row', 'col'), may hold values from -0.0546875 to 0.0546875
- vir_coeffs: bfloat16 [12000, 512], P('col', 'row'), may hold values from -0.0546875 to 0.0546875
- occ_energies: float32 [2000], replicated, may hold values from -1 to -0.1
- vir_energies: float32 [512], replicated, may hold values from 0.1 to 1.5
Outputs:
- density_response: bfloat16 [4, 12000, 12000], P('grp', 'row', 'col'), parts along dimension 0
There are 2 independent parts, one for each index of `grp`. A program takes and returns all parts, laid end to end along the dimension named above; an argument that names none is the same for every part. Nothing has to cross between parts.
All inputs are finite; a program needn't handle non-finite values.
Results may differ from a plain program's by a relative error of at most 0.0098.
Values may be sent and summed in bfloat16 or wider, within the bound.
A program may use at most 192 MiB of HBM per device.

v0:
```python
import jax
import jax.numpy as jnp
from jax import lax
from jax.sharding import PartitionSpec as P

BF16 = jnp.bfloat16
F32 = jnp.float32


def per_device(perturbation, occ_coeffs, vir_coeffs, occ_energies, vir_energies):
    vir_rows = lax.all_gather(vir_coeffs, "row", axis=1, tiled=True)
    occ_parts = lax.all_gather(occ_coeffs, "col")
    cols, _, width = occ_parts.shape
    image = jnp.einsum("pij,jv->piv", perturbation, vir_rows, preferred_element_type=F32).astype(
        BF16
    )
    part = jnp.einsum("cio,piv->pcov", occ_parts, image, preferred_element_type=F32).astype(BF16)
    coupling = lax.psum(part, ("row", "col"))
    gaps = occ_energies.reshape(cols, width)[:, :, None] - vir_energies[None, None, :]
    response = (coupling.astype(F32) / gaps[None]).astype(BF16)
    mixed = jnp.einsum("cio,pcov->piv", occ_parts, response, preferred_element_type=F32).astype(
        BF16
    )
    return jnp.einsum("piv,jv->pij", mixed, vir_rows, preferred_element_type=F32).astype(BF16)


def solution(mesh):
    placed = (P("grp", "row", "col"), P("row", "col"), P("col", "row"), P(), P())
    return jax.shard_map(
        per_device, mesh=mesh, in_specs=placed, out_specs=P("grp", "row", "col"), check_vma=False
    )
```

profile of v0, /device:TPU:0, one launch (start us, length us, event | category | flops | bytes accessed | tf_op | source)
XLA Modules:
  0.0 448.0 jit_solution(10581064769501468559)
XLA Ops:
  6.5 0.0 all-gather.4.cloned.1.call-start
  6.5 0.7 all-gather.4.cloned.1.call-update
  7.3 0.0 all-gather.6.cloned.1.call-start
  7.3 0.7 all-gather.6.cloned.1.call-update
  8.0 0.0 all-reduce.2.cloned.1.call-start
  8.1 32.1 %all-gather.4.cloned.1.call-done = bf16[3000,512]{1,0:T(8,128)(2,1)} async-done(((bf16[3000,128]{1,0:T(8,128)(2,1)}), bf16[3000,512]{1,0:T(8,128)(2,1)}) %all-gather.4.cloned.1.call-update) | async-done | bytes 3072016 | tf_op jit(solution)/shard_map/all_gather | solution.py:11
  40.1 25.8 %fusion.45 = bf16[2,3000,512,1]{2,1,3,0:T(8,128)(2,1)} fusion(bf16[2,3000,3000]{2,1,0:T(8,128)(2,1)} %param.5, bf16[3000,512]{1,0:T(8,128)(2,1)} %all-gather.4.cloned.1.call-done), kind=kOutput, calls=%fused_computation.5.clone.clone.clone.1 | convolution fusion | flops 18435072000 | bytes 45216000 | tf_op jit(solution)/shard_map/pij,jv->piv/dot_general | solution.py:14
  66.0 189.1 %all-gather.6.cloned.1.call-done = bf16[12000,500]{1,0:T(8,128)(2,1)} async-done(((bf16[3000,500]{1,0:T(8,128)(2,1)}), bf16[12000,500]{1,0:T(8,128)(2,1)}) %all-gather.6.cloned.1.call-update) | async-done | bytes 12000016 | tf_op jit(solution)/shard_map/all_gather | solution.py:12
  255.1 19.1 %fusion.17 = bf16[2,512,4,500]{1,3,2,0:T(8,128)(2,1)} fusion(bf16[4,3000,500,1]{2,1,0,3:T(8,128)(2,1)} %bitcast.58, bf16[2,3000,512,1]{2,1,3,0:T(8,128)(2,1)} %fusion.45), kind=kOutput, calls=%fused_computation.12 | convolution fusion | flops 12290048000 | bytes 22240000 | tf_op jit(solution)/shard_map/cio,piv->pcov/dot_general | solution.py:17
  274.2 0.0 copy-start
  274.2 0.0 copy-start.1
  274.2 7.8 %copy.10 = bf16[2,512,4,500]{3,2,1,0:T(4,128)(2,1)} copy(bf16[2,512,4,500]{1,3,2,0:T(8,128)(2,1)} %fusion.17) | data formatting | bytes 8192000
  282.0 0.0 all-reduce.2.cloned.1.call-update
  282.0 0.0 copy-done
  282.1 0.1 sub.19
  282.1 0.0 copy-done.1
  282.1 2.8 broadcast_subtract_fusion
  285.0 106.6 %all-reduce.2.cloned.1.call-done = bf16[2,4,500,512]{2,1,3,0:T(4,128)(2,1)} async-done(((bf16[2,4,500,512]{2,1,3,0:T(4,128)(2,1)}), bf16[2,4,500,512]{2,1,3,0:T(4,128)(2,1)}) %all-reduce.2.cloned.1.call-update) | async-done | bytes 4096016 | tf_op jit(solution)/shard_map/psum | solution.py:18
  391.5 5.5 %fusion = bf16[2,4,500,512]{2,1,3,0:T(4,128)(2,1)S(1)} fusion(bf16[2,4,500,512]{2,1,3,0:T(4,128)(2,1)} %all-reduce.2.cloned.1.call-done, f32[4,500,512]{1,0,2:T(4,128)} %broadcast_subtract_fusion), kind=kLoop, calls=%fused_computation.3 | loop fusion | flops 6144000 | bytes 12288000 | tf_op jit(solution)/shard_map/convert_element_type | solution.py:20
  397.1 16.8 %fusion.41 = bf16[2,3000,512]{2,1,0:T(8,128)(2,1)} fusion(bf16[4,3000,500,1]{2,1,0,3:T(8,128)(2,1)} %bitcast.59, bf16[2,4,500,512]{2,1,3,0:T(4,128)(2,1)S(1)} %fusion), kind=kOutput, calls=%fused_computation.6.clone.1 | convolution fusion | flops 12291072000 | bytes 22240000 | tf_op jit(solution)/shard_map/cio,pcov->piv/dot_general | solution.py:21
  413.9 27.6 %convolution_convert_fusion = bf16[2,3000,3000]{2,1,0:T(8,128)(2,1)} fusion(bf16[3000,512]{1,0:T(8,128)(2,1)} %all-gather.4.cloned.1.call-done, bf16[2,3000,512]{2,1,0:T(8,128)(2,1)} %fusion.41), kind=kOutput, calls=%fused_computation | convolution fusion | flops 18449999872 | bytes 45216000 | tf_op jit(solution)/shard_map/piv,jv->pij/dot_general | solution.py:24
Async XLA Ops:
  6.5 33.6 %all-gather.4.cloned.1.call-start = ((), (), s32[]{:S(2)}) async-start(), calls=%async_computation | async-start | bytes 3840000 | tf_op jit(solution)/shard_map/all_gather | solution.py:11
  7.3 247.8 %all-gather.6.cloned.1.call-start = ((), (), s32[]{:S(2)}) async-start(), calls=%async_computation.2 | async-start | bytes 15360000 | tf_op jit(solution)/shard_map/all_gather | solution.py:12
  8.0 383.5 %all-reduce.2.cloned.1.call-start = ((), (), s32[]{:S(2)}) async-start(), calls=%async_computation.1 | async-start | bytes 8388608 | tf_op jit(solution)/shard_map/psum | solution.py:18
  274.2 7.9 %copy-start = (f32[2000]{0:T(1024)S(1)}, f32[2000]{0:T(1024)}, u32[]{:S(2)}) copy-start(f32[2000]{0:T(1024)} %param.8) | copy-start | bytes 24004
  274.2 8.0 %copy-start.1 = (f32[512]{0:T(512)S(1)}, f32[512]{0:T(512)}, u32[]{:S(2)}) copy-start(f32[512]{0:T(512)} %param.9) | copy-start | bytes 6148
Sparse Core Ops, SparseCore 0:
  8.9 31.1 all-gather.3
  41.7 213.3 all-gather.5
  282.2 109.3 all-reduce.1
where the time goes:
time: 448 us
  waiting for transfers between devices  329 us (73%)
  matrix products  89.4 us (20%)
  between operations  13.1 us (3%)
  other arithmetic  8.38 us (2%)
  local copies, waits for them, and re-layouts  7.93 us (2%)
    all_gather x1, waiting for transfers between devices, per_device(): occ_parts = lax.all_gather(occ_coeffs, 'col')  189 us
    psum x1, waiting for transfers between devices, per_device(): coupling = lax.psum(part, ('row', 'col'))  107 us
    all_gather x1, waiting for transfers between devices, per_device(): vir_rows = lax.all_gather(vir_coeffs, 'row', axis=1, tiled=True)  32.1 us
    dot_general x1, matrix products, per_device(): jnp.einsum('piv,jv->pij', mixed, vir_rows, preferred_element_type=F32)  27.6 us
    dot_general x1, matrix products, per_device(): jnp.einsum('pij,jv->piv', perturbation, vir_rows, preferred_element_type=...  25.8 us
    dot_general x1, matrix products, per_device(): jnp.einsum('cio,piv->pcov', occ_parts, image, preferred_element_type=F32)  19.1 us
    dot_general x1, matrix products, per_device(): jnp.einsum('cio,pcov->piv', occ_parts, response, preferred_element_type=F32)  16.8 us
  transfers between devices with their start and end apart: 3, of which 3 were waited for; matrix products, arithmetic and copies ran while one was open for 6% of the time, Pallas kernels for 0%

commit v1 on v0

--- a/solution.py
+++ b/solution.py
@@ -15,7 +15,7 @@
         BF16
     )
     part = jnp.einsum("cio,piv->pcov", occ_parts, image, preferred_element_type=F32).astype(BF16)
-    coupling = lax.psum(part, ("row", "col"))
+    coupling = jnp.sum(lax.all_gather(part, ("row", "col")), axis=0)
     gaps = occ_energies.reshape(cols, width)[:, :, None] - vir_energies[None, None, :]
     response = (coupling.astype(F32) / gaps[None]).astype(BF16)
     mixed = jnp.einsum("cio,pcov->piv", occ_parts, response, preferred_element_type=F32).astype(

time: 448 us -> 705 us (1.57)
  waiting for transfers between devices: 329 us -> 556 us
  other arithmetic: 8.38 us -> 47.9 us
    all_gather x0 -> x1, waiting for transfers between devices: none -> 334 us  [per_device(): coupling = jnp.sum(lax.all_gather(part, ('row', 'col')), axis=0)]
    psum x1 -> x0, waiting for transfers between devices: 107 us -> none  [per_device(): coupling = lax.psum(part, ('row', 'col'))]
    reduce_sum x0 -> x1, other arithmetic: none -> 37.7 us  [per_device(): coupling = jnp.sum(lax.all_gather(part, ('row', 'col')), axis=0)]
    dot_general x1 -> x0, matrix products: 16.8 us -> none  [per_device(): jnp.einsum('cio,pcov->piv', occ_parts, response, preferred_element_type=F32)]
    dot_general x1, matrix products: 27.6 us -> 39.8 us  [per_device(): jnp.einsum('piv,jv->pij', mixed, vir_rows, preferred_element_type=F32)]
    unnamed x5 -> x6, local copies, waits for them, and re-layouts: 7.85 us -> 0.02 us
  transfers between devices with their start and end apart: 3 -> 3, of which waited for: 3 -> 3; matrix products, arithmetic and copies ran while one was open for 6% -> 4% of each run, Pallas kernels for 0% -> 0%
where the time goes in v1:
time: 705 us
  waiting for transfers between devices  556 us (79%)
  matrix products  82.9 us (12%)
  other arithmetic  47.9 us (7%)
  between operations  13.2 us (2%)
    all_gather x1, waiting for transfers between devices, per_device(): coupling = jnp.sum(lax.all_gather(part, ('row', 'col')), axis=0)  334 us
    all_gather x1, waiting for transfers between devices, per_device(): occ_parts = lax.all_gather(occ_coeffs, 'col')  189 us
    dot_general x1, matrix products, per_device(): jnp.einsum('piv,jv->pij', mixed, vir_rows, preferred_element_type=F32)  39.8 us
    reduce_sum x1, other arithmetic, per_device(): coupling = jnp.sum(lax.all_gather(part, ('row', 'col')), axis=0)  37.7 us
    all_gather x1, waiting for transfers between devices, per_device(): vir_rows = lax.all_gather(vir_coeffs, 'row', axis=1, tiled=True)  32.1 us
    dot_general x1, matrix products, per_device(): jnp.einsum('pij,jv->piv', perturbation, vir_rows, preferred_element_type=...  25.8 us
    dot_general x1, matrix products, per_device(): jnp.einsum('cio,piv->pcov', occ_parts, image, preferred_element_type=F32)  17.3 us
  transfers between devices with their start and end apart: 3, of which 3 were waited for; matrix products, arithmetic and copies ran while one was open for 4% of the time, Pallas kernels for 0%

profile of v1, /device:TPU:0, one launch (start us, length us, event | category | flops | bytes accessed | tf_op | source)
XLA Modules:
  0.0 704.9 jit_solution(371891771571585986)
XLA Ops:
  6.5 0.0 all-gather.6.cloned.1.call-start
  6.5 0.7 all-gather.6.cloned.1.call-update
  7.3 0.0 all-gather.8.cloned.1.call-start
  7.3 0.7 all-gather.8.cloned.1.call-update
  8.0 0.0 all-gather.10.cloned.1.call-start
  8.1 32.1 %all-gather.6.cloned.1.call-done = bf16[3000,512]{1,0:T(8,128)(2,1)} async-done(((bf16[3000,128]{1,0:T(8,128)(2,1)}), bf16[3000,512]{1,0:T(8,128)(2,1)}) %all-gather.6.cloned.1.call-update) | async-done | bytes 3072016 | tf_op jit(solution)/shard_map/all_gather | solution.py:11
  40.1 25.8 %fusion.40 = bf16[2,3000,512,1]{2,1,3,0:T(8,128)(2,1)} fusion(bf16[2,3000,3000]{2,1,0:T(8,128)(2,1)} %param.5, bf16[3000,512]{1,0:T(8,128)(2,1)} %all-gather.6.cloned.1.call-done), kind=kOutput, calls=%fused_computation.5.clone.clone.clone.1 | convolution fusion | flops 18435072000 | bytes 45216000 | tf_op jit(solution)/shard_map/pij,jv->piv/dot_general | solution.py:14
  65.9 189.2 %all-gather.8.cloned.1.call-done = bf16[12000,500]{1,0:T(8,128)(2,1)} async-done(((bf16[3000,500]{1,0:T(8,128)(2,1)}), bf16[12000,500]{1,0:T(8,128)(2,1)}) %all-gather.8.cloned.1.call-update) | async-done | bytes 12000016 | tf_op jit(solution)/shard_map/all_gather | solution.py:12
  255.1 17.3 %convert_bitcast_fusion = bf16[2,4,500,512]{3,2,1,0:T(8,128)(2,1)S(1)} fusion(bf16[4,3000,500,1]{2,1,0,3:T(8,128)(2,1)} %bitcast.57, bf16[2,3000,512,1]{2,1,3,0:T(8,128)(2,1)} %fusion.40), kind=kOutput, calls=%fused_computation.9 | convolution fusion | flops 12290048000 | bytes 22240000 | tf_op jit(solution)/shard_map/cio,piv->pcov/dot_general | solution.py:17
  272.4 0.0 copy-start
  272.4 0.0 copy-start.1
  272.4 4.1 copy.9
  276.5 0.0 all-gather.10.cloned.1.call-update
  276.5 0.0 copy-done
  276.5 0.1 sub.19
  276.6 0.1 copy.10
  276.8 0.0 copy-done.1
  276.8 2.8 broadcast_subtract_fusion
  279.6 333.8 %all-gather.10.cloned.1.call-done = bf16[32,4,500,512]{3,1,2,0:T(4,128)(2,1)} async-done(((bf16[2,4,500,512]{3,1,2,0:T(4,128)(2,1)}), bf16[32,4,500,512]{3,1,2,0:T(4,128)(2,1)}) %all-gather.10.cloned.1.call-update) | async-done | bytes 65536016 | tf_op jit(solution)/shard_map/all_gather | solution.py:18
  613.4 37.7 %reduce_sum.12 = bf16[2,4,500,512]{3,1,2,0:T(4,128)(2,1)} reduce(bf16[16,2,4,500,512]{4,2,3,1,0:T(4,128)(2,1)} %bitcast.56, bf16[]{:T(256)} %constant.2.clone.1), dimensions={0}, to_apply=%region_0.0 | reduce | flops 30720000 | bytes 69632000 | tf_op jit(solution)/shard_map/reduce_sum | solution.py:18
  651.1 0.0 copy-start.2
  651.1 7.5 %fusion = bf16[2,4,500,512]{3,1,2,0:T(4,128)(2,1)} fusion(bf16[2,4,500,512]{3,1,2,0:T(4,128)(2,1)} %reduce_sum.12, f32[4,500,512]{2,0,1:T(4,128)} %broadcast_subtract_fusion), kind=kLoop, calls=%fused_computation.3 | loop fusion | flops 6144000 | bytes 12288000 | tf_op jit(solution)/shard_map/convert_element_type | solution.py:20
  658.5 0.0 copy-done.2
  658.5 39.8 %convolution_convert_fusion = bf16[2,3000,3000]{2,1,0:T(8,128)(2,1)} fusion(bf16[4,3000,500,1]{2,1,0,3:T(8,128)(2,1)} %bitcast.58, bf16[2,4,500,512]{3,1,2,0:T(4,128)(2,1)} %fusion, bf16[3000,512]{1,0:T(8,128)(2,1)S(1)} %copy-done.2), kind=kOutput, calls=%fused_computation | convolution fusion | flops 30741071872 | bytes 55168000 | tf_op jit(solution)/shard_map/piv,jv->pij/dot_general | solution.py:24
Async XLA Ops:
  6.5 33.6 %all-gather.6.cloned.1.call-start = ((), (), s32[]{:S(2)}) async-start(), calls=%async_computation | async-start | bytes 3840000 | tf_op jit(solution)/shard_map/all_gather | solution.py:11
  7.3 247.8 %all-gather.8.cloned.1.call-start = ((), (), s32[]{:S(2)}) async-start(), calls=%async_computation.1 | async-start | bytes 15360000 | tf_op jit(solution)/shard_map/all_gather | solution.py:12
  8.0 605.4 %all-gather.10.cloned.1.call-start = ((), (), s32[]{:S(2)}) async-start(), calls=%async_computation.2 | async-start | bytes 69632000 | tf_op jit(solution)/shard_map/all_gather | solution.py:18
  272.4 4.1 copy-start
  272.4 4.4 copy-start.1
  651.1 7.5 %copy-start.2 = (bf16[3000,512]{1,0:T(8,128)(2,1)S(1)}, bf16[3000,512]{1,0:T(8,128)(2,1)}, u32[]{:S(2)}) copy-start(bf16[3000,512]{1,0:T(8,128)(2,1)} %all-gather.6.cloned.1.call-done) | copy-start | bytes 9216004
Sparse Core Ops, SparseCore 0:
  8.9 31.1 all-gather.5
  41.7 213.3 all-gather.7
  276.7 336.6 all-gather.9
